TPU v7x, 32 devices: a whole 2x2x4 slice. The times are simulated.
32 devices in a mesh: groups: 1, expert: 16 (over z, y, x), replica: 2 (over core).
Axes of the slice: x: 2, y: 2, z: 4, core: 2. Of those that a mesh axis runs over, the one named last changes fastest.
Arguments:
- queries: bfloat16 [128, 8192], P(('groups', 'expert', 'replica')), may hold values from -250 to 250
- token_keys: bfloat16 [128, 512], P(('groups', 'expert', 'replica')), may hold values from -6 to 6
- token_values: bfloat16 [128, 512], P(('groups', 'expert', 'replica')), may hold values from -6 to 6
- stored_keys: bfloat16 [128, 256, 512], P(('groups', 'expert', 'replica')), may hold values from -7 to 7
- stored_values: bfloat16 [128, 256, 512], P(('groups', 'expert', 'replica')), may hold values from -6 to 6
- kv_len: int32 [128], P(('groups', 'expert', 'replica')), may hold values from 2 to 256, as said below
- residual: bfloat16 [128, 4096], P(('groups', 'expert', 'replica')), may hold values from -6 to 6
- out_weight: bfloat16 [8192, 4096], P(('expert', 'replica')), may hold values from -0.1875 to 0.1875
- norm_gain: bfloat16 [4096], replicated, may hold values from 0.25 to 1.75
- expert_ids: int32 [128, 8], P(('groups', 'expert')), may hold values from 0 to 15, all different within a row; in each aligned block of 8 rows (0 to 7, 8 to 15, ...) at most 4 rows name the same one
- route_weight: float32 [128, 8], P(('groups', 'expert')), may hold values from 0.05 to 1
- w_gate: bfloat16 [16, 4096, 768], P('expert', None, 'replica'), may hold values from -0.09375 to 0.09375
- w_up: bfloat16 [16, 4096, 768], P('expert', None, 'replica'), may hold values from -0.09375 to 0.09375
- w_down: bfloat16 [16, 768, 4096], P('expert', 'replica'), may hold values from -0.4375 to 0.4375
Outputs:
- updated: bfloat16 [128, 4096], P(('groups', 'expert', 'replica'))
Inputs may be any that keep to these rules, and one draw needn't show every extreme that they name: `kv_len`: at least 2; some sequence uses all 256 positions. `expert_ids`: each token names 8 different experts; in each aligned block of 8 tokens no expert is named by more than 4 tokens, and some block reaches it.
All inputs are finite; a program needn't handle non-finite values.
Results may differ from a plain program's by a relative error of at most 0.01.
Values may be sent and summed in bfloat16 or wider, within the bound.
A program may use at most 64 MiB of HBM per device.

v0:
```python
import math

import jax
import jax.numpy as jnp
from jax import lax
from jax.sharding import PartitionSpec as P

HEAD_WIDTH = 128


def shifted(block, axis, distance):
    devices = range(lax.axis_size(axis))
    route = [(i - distance, i) for i in devices if i - distance in devices]
    return lax.ppermute(block, axis, route)


def attend_local(queries, token_keys, token_values, stored_keys, stored_values, kv_len):
    seq_count = queries.shape[0]
    cache_len = stored_keys.shape[1]
    kv_count = token_keys.shape[1] // HEAD_WIDTH
    query_group_width = queries.shape[1] // HEAD_WIDTH // kv_count
    query_head_rows = queries.reshape(seq_count, kv_count, query_group_width, HEAD_WIDTH)
    keys_from_cache = stored_keys.reshape(seq_count, cache_len, kv_count, HEAD_WIDTH)
    values_from_cache = stored_values.reshape(seq_count, cache_len, kv_count, HEAD_WIDTH)
    keys_latest = token_keys.reshape(seq_count, kv_count, HEAD_WIDTH)
    values_latest = token_values.astype(jnp.float32).reshape(seq_count, kv_count, HEAD_WIDTH)
    inv_root = 1.0 / math.sqrt(HEAD_WIDTH)
    cached_scores = (
        jnp.einsum(
            "bgqd,bpgd->bgqp", query_head_rows, keys_from_cache, preferred_element_type=jnp.float32
        )
        * inv_root
    )
    positions = lax.broadcasted_iota(jnp.int32, (seq_count, cache_len), 1)
    visible = positions < kv_len[:, None]
    cached_scores = jnp.where(visible[:, None, None, :], cached_scores, -jnp.inf)
    fresh_score = (
        jnp.einsum(
            "bgqd,bgd->bgq", query_head_rows, keys_latest, preferred_element_type=jnp.float32
        )
        * inv_root
    )
    highest = jnp.maximum(jnp.max(cached_scores, axis=-1), fresh_score)
    cached_exp = jnp.exp(cached_scores - highest[..., None])
    fresh_exp = jnp.exp(fresh_score - highest)
    totals = jnp.sum(cached_exp, axis=-1) + fresh_exp
    cached_prob = (cached_exp / totals[..., None]).astype(jnp.bfloat16)
    fresh_prob = lax.optimization_barrier((fresh_exp / totals).astype(jnp.bfloat16)).astype(
        jnp.float32
    )
    mixed = jnp.einsum(
        "bgqp,bpgd->bgqd", cached_prob, values_from_cache, preferred_element_type=jnp.float32
    )
    mixed = mixed + fresh_prob[..., None] * values_latest[:, :, None, :]
    return mixed.reshape(seq_count, -1).astype(jnp.bfloat16)


def on_device(
    queries,
    token_keys,
    token_values,
    stored_keys,
    stored_values,
    kv_len,
    residual,
    out_weight,
    norm_gain,
    expert_ids,
    route_weight,
    w_gate,
    w_up,
    w_down,
):
    attended = attend_local(queries, token_keys, token_values, stored_keys, stored_values, kv_len)
    column_groups = 8
    device_count = lax.axis_size(("expert", "replica"))
    seq_count, feature_total = attended.shape
    row_count, model_width = out_weight.shape
    feature_groups = device_count // column_groups
    feature_block = feature_total // feature_groups
    col_width = model_width // column_groups
    device_rank = lax.axis_index(("expert", "replica"))
    block_place = device_rank % column_groups
    slot_ids = jnp.arange(column_groups, dtype=jnp.int32)
    own_piece = lax.dynamic_slice_in_dim(out_weight, block_place * col_width, col_width, 1)
    empty_block = jnp.zeros((column_groups, row_count, col_width), out_weight.dtype)
    stacked = jnp.where((slot_ids == block_place)[:, None, None], own_piece[None], empty_block)
    for offset in range(1 - column_groups, column_groups):
        if offset != 0:
            target_place = (device_rank + offset) % column_groups
            sent_piece = lax.dynamic_slice_in_dim(
                out_weight, target_place * col_width, col_width, 1
            )
            arrived_piece = shifted(sent_piece, ("expert", "replica"), offset)
            stacked = jnp.where(
                (slot_ids == block_place - offset)[:, None, None], arrived_piece[None], stacked
            )
    weight_block = stacked.reshape(column_groups * row_count, col_width)
    repeated = jnp.repeat(
        attended.reshape(seq_count, feature_groups, feature_block), column_groups, axis=1
    )
    all_tokens = lax.all_to_all(
        repeated, ("expert", "replica"), split_axis=1, concat_axis=0, tiled=True
    )
    all_tokens = all_tokens.reshape(-1, feature_block)
    partial_cols = jnp.dot(all_tokens, weight_block, preferred_element_type=jnp.float32)
    partial_cols = partial_cols.reshape(-1, 1, col_width)
    came_back = lax.all_to_all(
        partial_cols.astype(jnp.bfloat16),
        ("expert", "replica"),
        split_axis=0,
        concat_axis=1,
        tiled=True,
    ).astype(partial_cols.dtype)
    projected = jnp.sum(
        came_back.reshape(seq_count, feature_groups, column_groups, col_width), axis=1
    ).reshape(seq_count, model_width)
    hidden_state = residual.astype(jnp.float32) + projected
    mean_square = jnp.mean(hidden_state * hidden_state, axis=-1, keepdims=True)
    normed = (hidden_state * lax.rsqrt(mean_square + 1e-06) * norm_gain.astype(jnp.float32)).astype(
        jnp.bfloat16
    )
    pair_tokens = lax.all_gather(normed, "replica", axis=0, tiled=True)
    token_count, topk_count = expert_ids.shape
    expert_count = lax.axis_size("expert")
    capacity = max(2, -(-(token_count * topk_count) // expert_count))
    flat_ids = expert_ids.reshape(-1)
    row_total = flat_ids.shape[0]
    same_expert = flat_ids[:, None] == flat_ids[None, :]
    row_iota = lax.broadcasted_iota(jnp.int32, (row_total, row_total), 0)
    col_iota = lax.broadcasted_iota(jnp.int32, (row_total, row_total), 1)
    slot_ranks = jnp.sum(jnp.where(same_expert & (col_iota < row_iota), 1, 0), axis=1).astype(
        jnp.int32
    )
    slot_of = (flat_ids * capacity + slot_ranks).reshape(token_count, topk_count)
    slot_total = expert_count * capacity
    slot_iota = jnp.arange(slot_total, dtype=jnp.int32)
    slot_hits = slot_of[None, :, :] == slot_iota[:, None, None]
    pick_table = jnp.sum(slot_hits.astype(jnp.float32), axis=2).astype(jnp.bfloat16)
    outgoing = jnp.dot(pick_table, pair_tokens, preferred_element_type=jnp.float32).astype(
        jnp.bfloat16
    )
    outgoing = outgoing.reshape(expert_count, capacity, -1)
    mixing = route_weight / jnp.sum(route_weight, axis=1, keepdims=True)
    combine_rows = jnp.sum(jnp.where(slot_hits, mixing[None, :, :], 0.0), axis=2).T
    incoming = lax.all_to_all(outgoing, "expert", split_axis=0, concat_axis=0, tiled=True)
    model_width = incoming.shape[-1]
    lead_shape = incoming.shape[:2]
    slot_rows = incoming.reshape(-1, model_width)
    gate_act = jnp.dot(slot_rows, w_gate[0], preferred_element_type=jnp.float32)
    up_act = jnp.dot(slot_rows, w_up[0], preferred_element_type=jnp.float32)
    hidden_act = (jax.nn.silu(gate_act) * up_act).astype(jnp.bfloat16)
    partial_value = jnp.dot(hidden_act, w_down[0], preferred_element_type=jnp.float32).reshape(
        lead_shape + (model_width,)
    )
    summed_halves = lax.psum(partial_value.astype(jnp.bfloat16), "replica").astype(jnp.float32)
    arrived = lax.all_to_all(
        summed_halves.astype(jnp.bfloat16), "expert", split_axis=0, concat_axis=0, tiled=True
    ).astype(summed_halves.dtype)
    returned = arrived
    returned = returned.reshape(slot_total, -1)
    seq_count = normed.shape[0]
    own_rows = lax.dynamic_slice_in_dim(
        combine_rows, lax.axis_index("replica") * seq_count, seq_count, 0
    )
    moe_out = jnp.dot(
        own_rows, returned, precision=lax.Precision.HIGHEST, preferred_element_type=jnp.float32
    )
    return (hidden_state + moe_out).astype(jnp.bfloat16)


def solution(mesh):
    in_specs = (
        P(("groups", "expert", "replica"), None),
        P(("groups", "expert", "replica"), None),
        P(("groups", "expert", "replica"), None),
        P(("groups", "expert", "replica"), None, None),
        P(("groups", "expert", "replica"), None, None),
        P(("groups", "expert", "replica")),
        P(("groups", "expert", "replica"), None),
        P(("expert", "replica"), None),
        P(),
        P(("groups", "expert"), None),
        P(("groups", "expert"), None),
        P("expert", None, "replica"),
        P("expert", None, "replica"),
        P("expert", "replica", None),
    )
    out_specs = P(("groups", "expert", "replica"), None)
    return jax.shard_map(
        on_device, mesh=mesh, in_specs=in_specs, out_specs=out_specs, check_vma=False
    )
```

profile of v0, /device:TPU:0, one launch (start us, length us, event | category | flops | bytes accessed | tf_op | source)
XLA Modules:
  0.0 200.0 jit_solution(9605539332392520658)
XLA Ops:
  6.6 4.1 %constant_dynamic-slice_fusion.15 = (bf16[256,512]{1,0:T(8,128)(2,1)}, bf16[256,512]{1,0:T(8,128)(2,1)}, bf16[256,512]{1,0:T(8,128)(2,1)}, bf16[256,512]{1,0:T(8...) fusion(bf16[256,4096]{1,0:T(8,128)(2,1)} %param.21, ...), kind=kLoop, calls=%fused_computation.59 | loop fusion | bytes 7864380 | tf_op jit(solution)/shard_map/dynamic_slice | solution.py:91
  10.7 6.0 %collective-permute-start = (bf16[256,512]{1,0:T(8,128)(2,1)}, bf16[256,512]{1,0:T(8,128)(2,1)}, u32[]{:S(2)}, u32[]{:S(2)}) collective-permute-start(bf16[256,512]{1,0:T(8,128)(2,1)} %get-tuple-element.7), channel_id=1, source_target_pairs={{0,7},{1,8},{2,9},{3,10},{4,11},{5,12},{6,13},{7,14},{8,15},{9,16}... | collective-permute-start | bytes 786440 | tf_op jit(solution)/shard_map/ppermute | solution.py:14
  16.7 4.1 %collective-permute-start.1 = (bf16[256,512]{1,0:T(8,128)(2,1)}, bf16[256,512]{1,0:T(8,128)(2,1)}, u32[]{:S(2)}, u32[]{:S(2)}) collective-permute-start(bf16[256,512]{1,0:T(8,128)(2,1)} %get-tuple-element.19), channel_id=1, source_target_pairs={{0,6},{1,7},{2,8},{3,9},{4,10},{5,11},{6,12},{7,13},{8,14},{9,15},... | collective-permute-start | bytes 786440 | tf_op jit(solution)/shard_map/ppermute | solution.py:14
  30.4 9.3 %all-to-all-start = ((bf16[4,32,2048]{2,0,1:T(4,128)(2,1)}), bf16[4,32,2048]{2,0,1:T(4,128)(2,1)}, u32[]{:S(2)}, u32[]{:S(2)}) async-start(bf16[4,32,2048]{2,0,1:T(4,128)(2,1)} %bitcast.67), calls=%async_computation | async-start | bytes 1048576 | tf_op jit(solution)/shard_map/all_to_all | solution.py:102
  41.1 4.0 %collective-permute-start.2 = (bf16[256,512]{1,0:T(8,128)(2,1)}, bf16[256,512]{1,0:T(8,128)(2,1)}, u32[]{:S(2)}, u32[]{:S(2)}) collective-permute-start(bf16[256,512]{1,0:T(8,128)(2,1)} %get-tuple-element.18), channel_id=1, source_target_pairs={{0,5},{1,6},{2,7},{3,8},{4,9},{5,10},{6,11},{7,12},{8,13},{9,14},{... | collective-permute-start | bytes 786440 | tf_op jit(solution)/shard_map/ppermute | solution.py:14
  45.2 6.2 %collective-permute-start.3 = (bf16[256,512]{1,0:T(8,128)(2,1)}, bf16[256,512]{1,0:T(8,128)(2,1)}, u32[]{:S(2)}, u32[]{:S(2)}) collective-permute-start(bf16[256,512]{1,0:T(8,128)(2,1)} %get-tuple-element.17), channel_id=1, source_target_pairs={{0,4},{1,5},{2,6},{3,7},{4,8},{5,9},{6,10},{7,11},{8,12},{9,13},{1... | collective-permute-start | bytes 786440 | tf_op jit(solution)/shard_map/ppermute | solution.py:14
  51.3 2.0 collective-permute-start.4
  53.6 4.2 %collective-permute-start.5 = (bf16[256,512]{1,0:T(8,128)(2,1)}, bf16[256,512]{1,0:T(8,128)(2,1)}, u32[]{:S(2)}, u32[]{:S(2)}) collective-permute-start(bf16[256,512]{1,0:T(8,128)(2,1)} %get-tuple-element.15), channel_id=1, source_target_pairs={{0,2},{1,3},{2,4},{3,5},{4,6},{5,7},{6,8},{7,9},{8,10},{9,11},{10,... | collective-permute-start | bytes 786440 | tf_op jit(solution)/shard_map/ppermute | solution.py:14
  57.9 2.0 %collective-permute-start.6 = (bf16[256,512]{1,0:T(8,128)(2,1)}, bf16[256,512]{1,0:T(8,128)(2,1)}, u32[]{:S(2)}, u32[]{:S(2)}) collective-permute-start(bf16[256,512]{1,0:T(8,128)(2,1)} %get-tuple-element.14), channel_id=1, source_target_pairs={{0,1},{1,2},{2,3},{3,4},{4,5},{5,6},{6,7},{7,8},{8,9},{9,10},{10,1... | collective-permute-start | bytes 786440 | tf_op jit(solution)/shard_map/ppermute | solution.py:14
  59.9 6.0 %collective-permute-done.2 = bf16[256,512]{1,0:T(8,128)(2,1)} collective-permute-done((bf16[256,512]{1,0:T(8,128)(2,1)}, bf16[256,512]{1,0:T(8,128)(2,1)}, u32[]{:S(2)}, u32[]{:S(2)}) %collective-permute-start.2) | collective-permute-done | bytes 262176 | tf_op jit(solution)/shard_map/ppermute | solution.py:14
  67.1 6.5 %collective-permute-done.3 = bf16[256,512]{1,0:T(8,128)(2,1)} collective-permute-done((bf16[256,512]{1,0:T(8,128)(2,1)}, bf16[256,512]{1,0:T(8,128)(2,1)}, u32[]{:S(2)}, u32[]{:S(2)}) %collective-permute-start.3) | collective-permute-done | bytes 262176 | tf_op jit(solution)/shard_map/ppermute | solution.py:14
  79.7 4.6 %collective-permute-done.8 = bf16[256,512]{1,0:T(8,128)(2,1)} collective-permute-done((bf16[256,512]{1,0:T(8,128)(2,1)}, bf16[256,512]{1,0:T(8,128)(2,1)}, u32[]{:S(2)}, u32[]{:S(2)}) %collective-permute-start.8) | collective-permute-done | bytes 262176 | tf_op jit(solution)/shard_map/ppermute | solution.py:14
  85.0 5.1 %select_select_fusion = bf16[8,256,512]{2,1,0:T(8,128)(2,1)} fusion(pred[8]{0:T(512)(128)(4,1)S(1)} %get-tuple-element.26, pred[8]{0:T(512)(128)(4,1)S(1)} %get-tuple-element.27, pred[8]{0:T(512)(128)(4,1)S(1)} %get-tuple-element.28, pred[8]{0:T(512)(128)(4,1)S(1)} %get-tuple-element.29, pred[8]{0:T(512)(128)(4,1)S(1)} %get-tuple-element.30, ...), kind=kLoop, calls=%fused_computation.9 | loop fusion | flops 15728640 | bytes 6029432 | tf_op jit(solution)/shard_map/jit(_where)/select_n | solution.py:95
  92.1 2.2 %fusion.7 = bf16[128,1,512]{2,0,1:T(8,128)(2,1)S(1)} fusion(bf16[128,2048]{1,0:T(8,128)(2,1)} %reshape.589, bf16[2048,512]{1,0:T(8,128)(2,1)} %bitcast.66), kind=kOutput, calls=%fused_computation.13 | convolution fusion | flops 268500992 | bytes 2752512 | tf_op jit(solution)/shard_map/dot_general | solution.py:106
  96.3 7.8 %all-to-all-start.1 = ((bf16[32,2,1024]{2,1,0:T(2,128)(2,1)}), bf16[32,2,1024]{2,1,0:T(2,128)(2,1)S(1)}, u32[]{:S(2)}, u32[]{:S(2)}) async-start(bf16[32,2,1024]{2,1,0:T(2,128)(2,1)} %reshape.604), calls=%async_computation.1 | async-start | bytes 262144 | tf_op jit(solution)/shard_map/all_to_all | solution.py:108
  106.3 6.0 %all-to-all-done.1 = bf16[32,2,1024]{2,1,0:T(2,128)(2,1)S(1)} async-done(((bf16[32,2,1024]{2,1,0:T(2,128)(2,1)}), bf16[32,2,1024]{2,1,0:T(2,128)(2,1)S(1)}, u32[]{:S(2)}, u32[]{:S(2)}) %all-to-all-start.1) | async-done | bytes 131104 | tf_op jit(solution)/shard_map/all_to_all | solution.py:108
  118.3 2.0 %reshape.591 = bf16[16,4,4096]{2,1,0:T(4,128)(2,1)} reshape(bf16[64,4096]{1,0:T(8,128)(2,1)} %convolution_convert_fusion.1) | data formatting | bytes 1048576 | tf_op jit(solution)/shard_map/reshape | solution.py:143
  120.3 19.7 %all_to_all.34 = bf16[16,4,4096]{2,1,0:T(4,128)(2,1)} all-to-all(bf16[16,4,4096]{2,1,0:T(4,128)(2,1)} %reshape.591), channel_id=1, replica_groups=mesh['groups'=1,'expert'=16,'replica'=2] {'expert'}, dimensions={0} | all-to-all | bytes 1048576 | tf_op jit(solution)/shard_map/all_to_all | solution.py:146
  142.0 2.8 %fusion.4 = f32[64,384]{1,0:T(8,128)S(1)} fusion(bf16[64,4096]{1,0:T(8,128)(2,1)} %reshape.592, bf16[1,4096,384]{2,1,0:T(8,128)(2,1)} %param.25), kind=kOutput, calls=%fused_computation.7 | convolution fusion | flops 201326592 | bytes 3768320 | tf_op jit(solution)/shard_map/dot_general | solution.py:150
  147.3 17.3 %all-reduce.2.cloned.1.call-done = bf16[16,4,4096]{2,0,1:T(8,128)(2,1)} async-done(((bf16[16,4,4096]{2,0,1:T(8,128)(2,1)}), bf16[16,4,4096]{2,0,1:T(8,128)(2,1)}) %all-reduce.2.cloned.1.call-update) | async-done | bytes 524304 | tf_op jit(solution)/shard_map/psum | solution.py:156
  164.6 2.2 %copy.34 = bf16[16,4,4096]{2,1,0:T(4,128)(2,1)} copy(bf16[16,4,4096]{2,0,1:T(8,128)(2,1)} %all-reduce.2.cloned.1.call-done) | data formatting | bytes 1048576 | tf_op jit(solution)/shard_map/psum | solution.py:156
  166.8 6.9 %all-to-all-start.3 = ((bf16[16,4,4096]{2,1,0:T(4,128)(2,1)}), bf16[16,4,4096]{2,1,0:T(4,128)(2,1)}, u32[]{:S(2)}, u32[]{:S(2)}) async-start(bf16[16,4,4096]{2,1,0:T(4,128)(2,1)} %copy.34), calls=%async_computation.3 | async-start | bytes 1048576 | tf_op jit(solution)/shard_map/all_to_all | solution.py:157
  173.7 15.5 %all-to-all-done.3 = bf16[16,4,4096]{2,1,0:T(4,128)(2,1)} async-done(((bf16[16,4,4096]{2,1,0:T(4,128)(2,1)}), bf16[16,4,4096]{2,1,0:T(4,128)(2,1)}, u32[]{:S(2)}, u32[]{:S(2)}) %all-to-all-start.3) | async-done | bytes 524320 | tf_op jit(solution)/shard_map/all_to_all | solution.py:157
  191.2 2.0 fusion
  (92 shorter events, 37.6 us)
Async XLA Ops:
  6.5 139.2 %copy-start = (bf16[1,384,4096]{2,1,0:T(8,128)(2,1)S(1)}, bf16[1,384,4096]{2,1,0:T(8,128)(2,1)}, u32[]{:S(2)}) copy-start(bf16[1,384,4096]{2,1,0:T(8,128)(2,1)} %param.27) | copy-start | bytes 9437188
  6.5 18.3 %copy-start.8 = (bf16[4,512]{1,0:T(4,128)(2,1)S(1)}, bf16[4,512]{1,0:T(4,128)(2,1)}, u32[]{:S(2)}) copy-start(bf16[4,512]{1,0:T(4,128)(2,1)} %param.15) | copy-start | bytes 12292
  6.5 21.1 %copy-start.9 = (bf16[4,512]{1,0:T(4,128)(2,1)S(1)}, bf16[4,512]{1,0:T(4,128)(2,1)}, u32[]{:S(2)}) copy-start(bf16[4,512]{1,0:T(4,128)(2,1)} %param.16) | copy-start | bytes 12292
  10.7 29.1 %collective-permute-start = (bf16[256,512]{1,0:T(8,128)(2,1)}, bf16[256,512]{1,0:T(8,128)(2,1)}, u32[]{:S(2)}, u32[]{:S(2)}) collective-permute-start(bf16[256,512]{1,0:T(8,128)(2,1)} %get-tuple-element.7), channel_id=1, source_target_pairs={{0,7},{1,8},{2,9},{3,10},{4,11},{5,12},{6,13},{7,14},{8,15},{9,16}... | collective-permute-start | bytes 786440 | tf_op jit(solution)/shard_map/ppermute | solution.py:14
  16.7 24.5 %collective-permute-start.1 = (bf16[256,512]{1,0:T(8,128)(2,1)}, bf16[256,512]{1,0:T(8,128)(2,1)}, u32[]{:S(2)}, u32[]{:S(2)}) collective-permute-start(bf16[256,512]{1,0:T(8,128)(2,1)} %get-tuple-element.19), channel_id=1, source_target_pairs={{0,6},{1,7},{2,8},{3,9},{4,10},{5,11},{6,12},{7,13},{8,14},{9,15},... | collective-permute-start | bytes 786440 | tf_op jit(solution)/shard_map/ppermute | solution.py:14
  20.8 24.4 %collective-permute-start.10 = (bf16[256,512]{1,0:T(8,128)(2,1)}, bf16[256,512]{1,0:T(8,128)(2,1)}, u32[]{:S(2)}, u32[]{:S(2)}) collective-permute-start(bf16[256,512]{1,0:T(8,128)(2,1)} %get-tuple-element.10), channel_id=1, source_target_pairs={{4,0},{5,1},{6,2},{7,3},{8,4},{9,5},{10,6},{11,7},{12,8},{13,9},{1... | collective-permute-start | bytes 786440 | tf_op jit(solution)/shard_map/ppermute | solution.py:14
  22.1 29.2 %collective-permute-start.11 = (bf16[256,512]{1,0:T(8,128)(2,1)}, bf16[256,512]{1,0:T(8,128)(2,1)}, u32[]{:S(2)}, u32[]{:S(2)}) collective-permute-start(bf16[256,512]{1,0:T(8,128)(2,1)} %get-tuple-element.9), channel_id=1, source_target_pairs={{5,0},{6,1},{7,2},{8,3},{9,4},{10,5},{11,6},{12,7},{13,8},{14,9},{... | collective-permute-start | bytes 786440 | tf_op jit(solution)/shard_map/ppermute | solution.py:14
  23.4 30.2 %collective-permute-start.12 = (bf16[256,512]{1,0:T(8,128)(2,1)}, bf16[256,512]{1,0:T(8,128)(2,1)}, u32[]{:S(2)}, u32[]{:S(2)}) collective-permute-start(bf16[256,512]{1,0:T(8,128)(2,1)} %get-tuple-element.8), channel_id=1, source_target_pairs={{6,0},{7,1},{8,2},{9,3},{10,4},{11,5},{12,6},{13,7},{14,8},{15,9},... | collective-permute-start | bytes 786440 | tf_op jit(solution)/shard_map/ppermute | solution.py:14
  27.7 25.7 %copy-start.6 = (s32[8,8]{1,0:T(8,128)S(1)}, s32[8,8]{1,0:T(8,128)}, u32[]{:S(2)}) copy-start(s32[8,8]{1,0:T(8,128)} %param.23) | copy-start | bytes 772
  30.4 59.6 %all-to-all-start = ((bf16[4,32,2048]{2,0,1:T(4,128)(2,1)}), bf16[4,32,2048]{2,0,1:T(4,128)(2,1)}, u32[]{:S(2)}, u32[]{:S(2)}) async-start(bf16[4,32,2048]{2,0,1:T(4,128)(2,1)} %bitcast.67), calls=%async_computation | async-start | bytes 1048576 | tf_op jit(solution)/shard_map/all_to_all | solution.py:102
  39.8 18.0 %collective-permute-start.13 = (bf16[256,512]{1,0:T(8,128)(2,1)}, bf16[256,512]{1,0:T(8,128)(2,1)}, u32[]{:S(2)}, u32[]{:S(2)}) collective-permute-start(bf16[256,512]{1,0:T(8,128)(2,1)} %get-tuple-element.21), channel_id=1, source_target_pairs={{7,0},{8,1},{9,2},{10,3},{11,4},{12,5},{13,6},{14,7},{15,8},{16,9}... | collective-permute-start | bytes 786440 | tf_op jit(solution)/shard_map/ppermute | solution.py:14
  41.1 24.7 %collective-permute-start.2 = (bf16[256,512]{1,0:T(8,128)(2,1)}, bf16[256,512]{1,0:T(8,128)(2,1)}, u32[]{:S(2)}, u32[]{:S(2)}) collective-permute-start(bf16[256,512]{1,0:T(8,128)(2,1)} %get-tuple-element.18), channel_id=1, source_target_pairs={{0,5},{1,6},{2,7},{3,8},{4,9},{5,10},{6,11},{7,12},{8,13},{9,14},{... | collective-permute-start | bytes 786440 | tf_op jit(solution)/shard_map/ppermute | solution.py:14
  45.2 28.4 %collective-permute-start.3 = (bf16[256,512]{1,0:T(8,128)(2,1)}, bf16[256,512]{1,0:T(8,128)(2,1)}, u32[]{:S(2)}, u32[]{:S(2)}) collective-permute-start(bf16[256,512]{1,0:T(8,128)(2,1)} %get-tuple-element.17), channel_id=1, source_target_pairs={{0,4},{1,5},{2,6},{3,7},{4,8},{5,9},{6,10},{7,11},{8,12},{9,13},{1... | collective-permute-start | bytes 786440 | tf_op jit(solution)/shard_map/ppermute | solution.py:14
  51.3 23.6 %collective-permute-start.4 = (bf16[256,512]{1,0:T(8,128)(2,1)}, bf16[256,512]{1,0:T(8,128)(2,1)}, u32[]{:S(2)}, u32[]{:S(2)}) collective-permute-start(bf16[256,512]{1,0:T(8,128)(2,1)} %get-tuple-element.16), channel_id=1, source_target_pairs={{0,3},{1,4},{2,5},{3,6},{4,7},{5,8},{6,9},{7,10},{8,11},{9,12},{10... | collective-permute-start | bytes 786440 | tf_op jit(solution)/shard_map/ppermute | solution.py:14
  53.6 26.0 %collective-permute-start.5 = (bf16[256,512]{1,0:T(8,128)(2,1)}, bf16[256,512]{1,0:T(8,128)(2,1)}, u32[]{:S(2)}, u32[]{:S(2)}) collective-permute-start(bf16[256,512]{1,0:T(8,128)(2,1)} %get-tuple-element.15), channel_id=1, source_target_pairs={{0,2},{1,3},{2,4},{3,5},{4,6},{5,7},{6,8},{7,9},{8,10},{9,11},{10,... | collective-permute-start | bytes 786440 | tf_op jit(solution)/shard_map/ppermute | solution.py:14
  57.9 21.8 %collective-permute-start.6 = (bf16[256,512]{1,0:T(8,128)(2,1)}, bf16[256,512]{1,0:T(8,128)(2,1)}, u32[]{:S(2)}, u32[]{:S(2)}) collective-permute-start(bf16[256,512]{1,0:T(8,128)(2,1)} %get-tuple-element.14), channel_id=1, source_target_pairs={{0,1},{1,2},{2,3},{3,4},{4,5},{5,6},{6,7},{7,8},{8,9},{9,10},{10,1... | collective-permute-start | bytes 786440 | tf_op jit(solution)/shard_map/ppermute | solution.py:14
  65.9 13.8 %collective-permute-start.7 = (bf16[256,512]{1,0:T(8,128)(2,1)}, bf16[256,512]{1,0:T(8,128)(2,1)}, u32[]{:S(2)}, u32[]{:S(2)}) collective-permute-start(bf16[256,512]{1,0:T(8,128)(2,1)} %get-tuple-element.13), channel_id=1, source_target_pairs={{1,0},{2,1},{3,2},{4,3},{5,4},{6,5},{7,6},{8,7},{9,8},{10,9},{11,1... | collective-permute-start | bytes 786440 | tf_op jit(solution)/shard_map/ppermute | solution.py:14
  73.6 10.6 %collective-permute-start.8 = (bf16[256,512]{1,0:T(8,128)(2,1)}, bf16[256,512]{1,0:T(8,128)(2,1)}, u32[]{:S(2)}, u32[]{:S(2)}) collective-permute-start(bf16[256,512]{1,0:T(8,128)(2,1)} %get-tuple-element.12), channel_id=1, source_target_pairs={{2,0},{3,1},{4,2},{5,3},{6,4},{7,5},{8,6},{9,7},{10,8},{11,9},{12,... | collective-permute-start | bytes 786440 | tf_op jit(solution)/shard_map/ppermute | solution.py:14
  74.9 10.1 %collective-permute-start.9 = (bf16[256,512]{1,0:T(8,128)(2,1)}, bf16[256,512]{1,0:T(8,128)(2,1)}, u32[]{:S(2)}, u32[]{:S(2)}) collective-permute-start(bf16[256,512]{1,0:T(8,128)(2,1)} %get-tuple-element.11), channel_id=1, source_target_pairs={{3,0},{4,1},{5,2},{6,3},{7,4},{8,5},{9,6},{10,7},{11,8},{12,9},{13... | collective-permute-start | bytes 786440 | tf_op jit(solution)/shard_map/ppermute | solution.py:14
  96.3 16.1 %all-to-all-start.1 = ((bf16[32,2,1024]{2,1,0:T(2,128)(2,1)}), bf16[32,2,1024]{2,1,0:T(2,128)(2,1)S(1)}, u32[]{:S(2)}, u32[]{:S(2)}) async-start(bf16[32,2,1024]{2,1,0:T(2,128)(2,1)} %reshape.604), calls=%async_computation.1 | async-start | bytes 262144 | tf_op jit(solution)/shard_map/all_to_all | solution.py:108
  104.1 60.5 %all-reduce.2.cloned.1.call-start = ((), (), s32[]{:S(2)}) async-start(), calls=%async_computation.4 | async-start | bytes 1048576 | tf_op jit(solution)/shard_map/psum | solution.py:156
  147.2 44.0 %copy-start.4 = (bf16[4,4096]{1,0:T(4,128)(2,1)S(1)}, bf16[4,4096]{1,0:T(4,128)(2,1)}, u32[]{:S(2)}) copy-start(bf16[4,4096]{1,0:T(4,128)(2,1)} %param.20) | copy-start | bytes 98308
  147.2 44.0 %copy-start.7 = (f32[64,8]{0,1:T(8,128)S(1)}, f32[64,8]{0,1:T(8,128)}, u32[]{:S(2)}) copy-start(f32[64,8]{0,1:T(8,128)} %get-tuple-element.5) | copy-start | bytes 6148
  166.8 22.4 %all-to-all-start.3 = ((bf16[16,4,4096]{2,1,0:T(4,128)(2,1)}), bf16[16,4,4096]{2,1,0:T(4,128)(2,1)}, u32[]{:S(2)}, u32[]{:S(2)}) async-start(bf16[16,4,4096]{2,1,0:T(4,128)(2,1)} %copy.34), calls=%async_computation.3 | async-start | bytes 1048576 | tf_op jit(solution)/shard_map/all_to_all | solution.py:157
  (5 other events, 43.0 us)
Sparse Core Ops, SparseCore 0:
  147.4 17.1 all-reduce.1
where the time goes:
time: 202 us; the launch traced here: 200 us
  starting transfers between devices  61.6 us (30%)
  waiting for transfers between devices  56.7 us (28%)
  blocking collectives  21.6 us (11%)
  local copies, waits for them, and re-layouts  18.3 us (9%)
  matrix products  14.3 us (7%)
  other arithmetic  13.8 us (7%)
  between operations  13.8 us (7%)
    ppermute x14, starting transfers between devices, shifted(): return lax.ppermute(block, axis, route)  37.6 us
    all_to_all x1, blocking collectives, on_device(): lax.all_to_all(outgoing, 'expert', split_axis=0, concat_axis=0, tiled=True)  19.7 us
    ppermute x14, waiting for transfers between devices, shifted(): return lax.ppermute(block, axis, route)  17.8 us
    psum x1, waiting for transfers between devices, on_device(): lax.psum(partial_value.astype(jnp.bfloat16), 'replica').astype(jnp.float32)  17.3 us
    all_to_all x1, waiting for transfers between devices, on_device(): lax.all_to_all(summed_halves.astype(jnp.bfloat16), 'expert', split_axis=0...  15.5 us
    all_to_all x1, starting transfers between devices, on_device(): lax.all_to_all(repeated, ('expert', 'replica'), split_axis=1, concat_axis...  9.28 us
    all_to_all x1, starting transfers between devices, on_device(): lax.all_to_all(partial_cols.astype(jnp.bfloat16), ('expert', 'replica'),...  7.84 us
    all_to_all x1, starting transfers between devices, on_device(): lax.all_to_all(summed_halves.astype(jnp.bfloat16), 'expert', split_axis=0...  6.88 us
  transfers between devices with their start and end apart: 18, of which 7 were waited for; matrix products, arithmetic and copies ran while one was open for 8% of the time, Pallas kernels for 0%

commit v1 on v0

v1 whole, which is shorter than its diff:
```python
import functools
import math

import jax
import jax.numpy as jnp
from jax import lax
from jax.experimental import pallas as pl
from jax.experimental.pallas import tpu as pltpu
from jax.sharding import PartitionSpec as P

HEAD_WIDTH = 128
TILE = 16
MESH = pl.DeviceIdType.MESH
F32 = jnp.float32
BF16 = jnp.bfloat16


def regroup(outer, inner, back=False):
    size = 8 * outer * inner
    shape = (8 * TILE, size) if back else (size, 8 * TILE)
    a = lax.broadcasted_iota(jnp.int32, shape, 1 if back else 0)
    b = lax.broadcasted_iota(jnp.int32, shape, 0 if back else 1)
    o = a // (8 * inner)
    j = (a // inner) % 8
    i = a % inner
    return jnp.where(b == j * TILE + o * inner + i, 1.0, 0.0).astype(BF16)


def dot(a, b):
    return jnp.dot(a, b, preferred_element_type=F32)


def kernel(
    E, cap,
    q_ref, tk_ref, tv_ref, kv_ref, res_ref, gain_ref, ids_ref, rw_ref,
    k_hbm, v_hbm, ow_hbm, wg_hbm, wu_hbm, wd_hbm,
    out_ref,
    kb, vb, ow, wg, wu, wd,
    qs, tks, tvs, att, ratt, asm, yb, rs, resb, resp, hs, ssb, ssp,
    tts, whi, wlo, xb, xr, xs, hid, os, zb, zr, ub, up_,
    lsem, wsem, psend, precv, s1, r1, s2, r2, s3, r3, s4, r4,
):
    N = 2 * E
    e_me = lax.axis_index("expert")
    c = lax.axis_index("replica")
    rank = e_me * 2 + c
    S = q_ref.shape[0]
    T = 2 * S
    heads = q_ref.shape[1] // HEAD_WIDTH
    G = tk_ref.shape[1] // HEAD_WIDTH
    width = heads // G
    L = k_hbm.shape[1]
    D = res_ref.shape[1]
    half = D // 2
    hpc = heads // E
    Q = TILE // cap
    cw = half // Q
    mine = pl.ds(pl.multiple_of(c * half, half), half)
    other = pl.ds(pl.multiple_of((1 - c) * half, half), half)
    partner = {"expert": e_me, "replica": 1 - c}

    barrier = pltpu.get_barrier_semaphore()

    @pl.loop(1, N)
    def _(i):
        peer = lax.rem(rank + i, N)
        pl.semaphore_signal(
            barrier, inc=1,
            device_id={"expert": peer // 2, "replica": lax.rem(peer, 2)}, device_id_type=MESH,
        )

    kcopies = []
    for b in range(S):
        kcopies.append(pltpu.make_async_copy(k_hbm.at[b], kb.at[pl.ds(b * L, L)], lsem.at[b]))
    vcopies = []
    for b in range(S):
        vcopies.append(pltpu.make_async_copy(v_hbm.at[b], vb.at[pl.ds(b * L, L)], lsem.at[S + b]))
    for cp in kcopies + vcopies:
        cp.start()
    orow = ow_hbm.shape[0]
    drow = wd_hbm.shape[1]
    omine = pl.ds(pl.multiple_of(c * orow, orow), orow)
    dmine = pl.ds(pl.multiple_of(c * drow, drow), drow)
    wcopies = [
        pltpu.make_async_copy(ow_hbm.at[:, mine], ow.at[omine], wsem.at[0]),
        pltpu.make_async_copy(wg_hbm.at[0], wg, wsem.at[1]),
        pltpu.make_async_copy(wu_hbm.at[0], wu, wsem.at[2]),
        pltpu.make_async_copy(wd_hbm.at[0, :, mine], wd.at[dmine], wsem.at[3]),
    ]
    for cp in wcopies:
        cp.start()

    qf = q_ref[...].astype(F32)
    for h in range(heads):
        qs[pl.ds(S * h, S), :] = qf[:, h * HEAD_WIDTH:(h + 1) * HEAD_WIDTH]
    for rep in range(8 // S):
        tks[pl.ds(rep * S, S), :] = tk_ref[...].astype(F32)
        tvs[pl.ds(rep * S, S), :] = tv_ref[...].astype(F32)
        resb[pl.ds(rep * S, S), :] = res_ref[...].astype(F32)
    rows = S * width
    row = lax.broadcasted_iota(jnp.int32, (rows, S * L), 0)
    col = lax.broadcasted_iota(jnp.int32, (rows, S * L), 1)
    seq = col // L
    length = jnp.zeros((rows, S * L), jnp.int32)
    for b in range(S):
        length = jnp.where(seq == b, kv_ref[b], length)
    seen = (row % S == seq) & (col - seq * L < length)
    inv_root = 1.0 / math.sqrt(HEAD_WIDTH)
    for cp in kcopies + vcopies:
        cp.wait()
    for g in range(G):
        lanes = slice(g * HEAD_WIDTH, (g + 1) * HEAD_WIDTH)
        qg = qs[g * rows:(g + 1) * rows, :]
        score = lax.dot_general(
            qg.astype(BF16), kb[:, lanes], (((1,), (1,)), ((), ())), preferred_element_type=F32
        ) * inv_root
        score = jnp.where(seen, score, -jnp.inf)
        tk = tks[:, lanes]
        tv = tvs[:, lanes]
        fresh = jnp.sum(
            (qg.reshape(rows // 8, 8, HEAD_WIDTH) * tk[None]).reshape(rows, HEAD_WIDTH),
            axis=1, keepdims=True,
        ) * inv_root
        top = jnp.maximum(jnp.max(score, axis=1, keepdims=True), fresh)
        ex = jnp.exp(score - top)
        fex = jnp.exp(fresh - top)
        inv = 1.0 / (jnp.sum(ex, axis=1, keepdims=True) + fex)
        prob = (ex * inv).astype(BF16)
        fprob = (fex * inv).astype(BF16).astype(F32)
        o = dot(prob, vb[:, lanes])
        o = o + (
            fprob.reshape(rows // 8, 8, 1) * tv[None]
        ).reshape(rows, HEAD_WIDTH)
        per = hpc * S
        if per == TILE:
            att[g * rows:(g + 1) * rows, :] = o.astype(BF16)
        else:
            for j in range(rows // per):
                base = (g * (rows // per) + j) * TILE
                att[base:base + per, :] = o[j * per:(j + 1) * per].astype(BF16)

    pl.semaphore_wait(barrier, N - 1)

    def tile(ref, index):
        return ref.at[pl.ds(pl.multiple_of(index * TILE, TILE), TILE)]

    def att_copy(i, inbound=False):
        peer = lax.rem(rank + N - i, N) if inbound else lax.rem(rank + i, N)
        who = peer if inbound else rank
        return pltpu.make_async_remote_copy(
            src_ref=tile(att, peer // 2), dst_ref=tile(ratt, who),
            send_sem=s1.at[i], recv_sem=r1.at[who],
            device_id={"expert": peer // 2, "replica": lax.rem(peer, 2)}, device_id_type=MESH,
        )

    def spread(src, dst, send, recv, i, inbound=False):
        peer = lax.rem(e_me + E - i, E) if inbound else lax.rem(e_me + i, E)
        who = peer if inbound else e_me
        return pltpu.make_async_remote_copy(
            src_ref=tile(src, peer), dst_ref=tile(dst, who),
            send_sem=send.at[i], recv_sem=recv.at[who],
            device_id={"expert": peer, "replica": c}, device_id_type=MESH,
        )

    def beside(src, dst, k):
        return pltpu.make_async_remote_copy(
            src_ref=src, dst_ref=dst, send_sem=psend.at[k], recv_sem=precv.at[k],
            device_id=partner, device_id_type=MESH,
        )

    ow_x = beside(ow_hbm.at[:, other], ow.at[omine], 0)
    wd_x = beside(wd_hbm.at[0, :, other], wd.at[dmine], 1)
    res_x = beside(resb.at[:, other], resp, 2)
    ow_x.start()

    @pl.loop(1, N)
    def _(i):
        att_copy(i).start()

    own1 = pltpu.make_async_copy(tile(att, e_me), tile(ratt, rank), lsem.at[0])
    own1.start()
    res_x.start()
    wd_x.start()

    lanes_all = E * TILE
    lane = lax.broadcasted_iota(jnp.int32, (T, lanes_all), 1)
    tok = lax.broadcasted_iota(jnp.int32, (T, lanes_all), 0)
    le = lane // TILE
    lq = (lane // cap) % Q
    ls = lane % cap
    ids = ids_ref[...]
    rw = rw_ref[...]
    mix = rw / jnp.sum(rw, axis=1, keepdims=True)
    named = jnp.zeros((T, lanes_all), F32)
    weight = jnp.zeros((T, lanes_all), F32)
    for k in range(ids.shape[1]):
        hit = ids[:, k:k + 1] == le
        named = named + jnp.where(hit, 1.0, 0.0)
        weight = weight + jnp.where(hit, mix[:, k:k + 1], 0.0)
    before = jnp.zeros((T, lanes_all), F32)
    for t in range(T - 1):
        before = before + jnp.where(tok > t, named[t:t + 1, :], 0.0)
    chosen = jnp.where(before == ls.astype(F32), named, 0.0)
    weight = weight * chosen
    high = weight.astype(BF16).astype(F32)
    low = weight - high
    for p in range(Q):
        here = lq == p
        tts[p * T:(p + 1) * T, :] = jnp.where(here, chosen, 0.0)
        whi[p * T:(p + 1) * T, :] = jnp.where(here, high, 0.0)
        wlo[p * T:(p + 1) * T, :] = jnp.where(here, low, 0.0)

    wcopies[0].wait()
    ow_x.wait()
    own1.wait()

    @pl.loop(1, N)
    def _(i):
        att_copy(i, True).wait_recv()

    pa = regroup(hpc, S)
    for grp in range(N // 8):
        blk = dot(pa, ratt[grp * 8 * TILE:(grp + 1) * 8 * TILE, :]).astype(BF16)
        for h in range(hpc):
            asm[grp * 8 * S:(grp + 1) * 8 * S, h * HEAD_WIDTH:(h + 1) * HEAD_WIDTH] = (
                blk[h * 8 * S:(h + 1) * 8 * S]
            )
    quarter = half // 2
    step = min(512, quarter)
    for j in range(quarter // step):
        y0 = dot(asm[...], ow[:, j * step:(j + 1) * step])
        y1 = dot(asm[...], ow[:, quarter + j * step:quarter + (j + 1) * step])
        both = jnp.concatenate([y0.reshape(E, T, step), y1.reshape(E, T, step)], axis=1)
        yb[:, j * step:(j + 1) * step] = both.reshape(E * TILE, step).astype(BF16)

    @pl.loop(1, E)
    def _(i):
        spread(yb, rs, s2, r2, i).start()

    own2 = pltpu.make_async_copy(tile(yb, e_me), tile(rs, e_me), lsem.at[1])
    own2.start()
    res_x.wait()
    own2.wait()

    @pl.loop(1, E)
    def _(i):
        spread(yb, rs, s2, r2, i, True).wait_recv()

    total = rs[0:TILE, :].astype(F32)
    for j in range(1, E):
        total = total + rs[j * TILE:(j + 1) * TILE, :].astype(F32)
    projected = jnp.concatenate([total[:T], total[T:]], axis=1)
    trow = lax.broadcasted_iota(jnp.int32, (T, half), 0)
    own_token = trow // S == c
    hidden = jnp.where(own_token, resb[:, mine], resp[...]) + projected
    hs[...] = hidden
    square = jnp.sum(hidden * hidden, axis=1, keepdims=True)
    ssb[...] = jnp.broadcast_to(square, ssb.shape)
    ss_x = beside(ssb, ssp, 3)
    ss_x.start()
    scaled = hidden * gain_ref[:, mine].astype(F32)
    ss_x.wait()
    mean = (square + ssp[:, 0:1]) / D
    normed = scaled * lax.rsqrt(mean + 1e-06)
    stacked = jnp.concatenate([normed[:, p * cw:(p + 1) * cw] for p in range(Q)], axis=0)
    picked = lax.dot_general(
        tts[...].astype(BF16), stacked.astype(BF16), (((0,), (0,)), ((), ())),
        preferred_element_type=F32,
    )
    xb[...] = picked.astype(BF16)

    @pl.loop(1, E)
    def _(i):
        spread(xb, xr.at[c], s3, r3, i).start()

    own3 = pltpu.make_async_copy(tile(xb, e_me), tile(xr.at[c], e_me), lsem.at[2])
    own3.start()
    for cp in wcopies[1:]:
        cp.wait()
    wd_x.wait()
    own3.wait()

    @pl.loop(1, E)
    def _(i):
        spread(xb, xr.at[c], s3, r3, i, True).wait_recv()

    x_x = beside(xr.at[c], xr.at[c], 4)
    x_x.start()
    px = regroup(Q, cap)
    gc = 8 * cap
    gate = None
    for turn in range(2):
        side = c if turn == 0 else 1 - c
        if turn == 1:
            x_x.wait()
        for grp in range(E // 8):
            blk = dot(px, xr[side, grp * 8 * TILE:(grp + 1) * 8 * TILE, :]).astype(BF16)
            for p in range(Q):
                xs[turn, grp * gc:(grp + 1) * gc, p * cw:(p + 1) * cw] = blk[p * gc:(p + 1) * gc]
        feats = pl.ds(pl.multiple_of(side * half, half), half)
        gpart = dot(xs[turn], wg[feats, :])
        upart = dot(xs[turn], wu[feats, :])
        gate, up = (gpart, upart) if turn == 0 else (gate + gpart, up + upart)
    hid[c] = (gate / (1.0 + jnp.exp(-gate)) * up).astype(BF16)
    h_x = beside(hid.at[c], hid.at[c], 5)
    h_x.start()
    h_x.wait()
    for p in range(Q):
        cols = slice(p * cw, (p + 1) * cw)
        o = dot(hid[0], wd[0:drow, cols]) + dot(hid[1], wd[drow:2 * drow, cols])
        o = o.astype(BF16)
        for grp in range(E // 8):
            os[grp * 8 * TILE + p * gc:grp * 8 * TILE + (p + 1) * gc, :] = (
                o[grp * gc:(grp + 1) * gc]
            )
    pb = regroup(Q, cap, True)
    for grp in range(E // 8):
        part = slice(grp * 8 * TILE, (grp + 1) * 8 * TILE)
        zb[part, :] = dot(pb, os[part, :]).astype(BF16)

    @pl.loop(1, E)
    def _(i):
        spread(zb, zr, s4, r4, i).start()

    own4 = pltpu.make_async_copy(tile(zb, e_me), tile(zr, e_me), lsem.at[3])
    own4.start()
    own4.wait()

    @pl.loop(1, E)
    def _(i):
        spread(zb, zr, s4, r4, i, True).wait_recv()

    moe = dot(whi[...].astype(BF16), zr[...]) + dot(wlo[...].astype(BF16), zr[...])
    updated = hs[...] + jnp.concatenate([moe[p * T:(p + 1) * T] for p in range(Q)], axis=1)
    ub[...] = updated
    u_x = beside(ub, up_, 6)
    u_x.start()
    first = c == 0
    out_ref[:, mine] = jnp.where(first, updated[:S], updated[S:]).astype(BF16)
    u_x.wait()
    got = up_[...]
    out_ref[:, other] = jnp.where(first, got[:S], got[S:]).astype(BF16)

    @pl.loop(1, N)
    def _(i):
        att_copy(i).wait_send()

    @pl.loop(1, E)
    def _(i):
        spread(yb, rs, s2, r2, i).wait_send()
        spread(xb, xr.at[c], s3, r3, i).wait_send()
        spread(zb, zr, s4, r4, i).wait_send()


def on_device(
    queries, token_keys, token_values, stored_keys, stored_values, kv_len, residual, out_weight,
    norm_gain, expert_ids, route_weight, w_gate, w_up, w_down,
):
    E = lax.axis_size("expert")
    N = 2 * E
    S, features = queries.shape
    T = 2 * S
    L = stored_keys.shape[1]
    KW = token_keys.shape[1]
    D = residual.shape[1]
    half = D // 2
    topk = expert_ids.shape[1]
    FH = w_gate.shape[2]
    cap = max(2, -(-(T * topk) // E))
    Q = TILE // cap
    cw = half // Q
    orow = out_weight.shape[0]
    vmem = pl.BlockSpec(memory_space=pltpu.VMEM)
    smem = pl.BlockSpec(memory_space=pltpu.SMEM)
    hbm = pl.BlockSpec(memory_space=pl.ANY)
    V = pltpu.VMEM
    dma = pltpu.SemaphoreType.DMA
    scratch = [
        V((S * L, KW), BF16), V((S * L, KW), BF16),
        V((2 * orow, half), BF16), V((D, FH), BF16), V((D, FH), BF16), V((2 * FH, half), BF16),
        V((S * features // HEAD_WIDTH, HEAD_WIDTH), F32), V((8, KW), F32), V((8, KW), F32),
        V((E * TILE, HEAD_WIDTH), BF16), V((N * TILE, HEAD_WIDTH), BF16),
        V((N * S, 2 * orow), BF16),
        V((E * TILE, half // 2), BF16), V((E * TILE, half // 2), BF16),
        V((T, D), F32), V((T, half), F32), V((T, half), F32), V((T, 128), F32), V((T, 128), F32),
        V((Q * T, E * TILE), F32), V((Q * T, E * TILE), F32), V((Q * T, E * TILE), F32),
        V((E * TILE, cw), BF16), V((2, E * TILE, cw), BF16), V((2, E * cap, half), BF16),
        V((2, E * cap, FH), BF16),
        V((E * TILE, cw), BF16), V((E * TILE, cw), BF16), V((E * TILE, cw), BF16),
        V((T, half), F32), V((T, half), F32),
        dma((2 * S,)), dma((4,)), dma((7,)), dma((7,)),
        dma((N,)), dma((N,)), dma((E,)), dma((E,)), dma((E,)), dma((E,)), dma((E,)), dma((E,)),
    ]
    return pl.pallas_call(
        functools.partial(kernel, E, cap),
        out_shape=jax.ShapeDtypeStruct((S, D), BF16),
        in_specs=[vmem, vmem, vmem, smem, vmem, vmem, vmem, vmem, hbm, hbm, hbm, hbm, hbm, hbm],
        out_specs=vmem,
        scratch_shapes=scratch,
        compiler_params=pltpu.CompilerParams(
            collective_id=0, has_side_effects=True, vmem_limit_bytes=48 * 1024 * 1024
        ),
    )(
        queries, token_keys, token_values, kv_len, residual, norm_gain.reshape(1, D), expert_ids,
        route_weight, stored_keys, stored_values, out_weight, w_gate, w_up, w_down,
    )


def solution(mesh):
    rows = P(("groups", "expert", "replica"), None)
    cube = P(("groups", "expert", "replica"), None, None)
    in_specs = (
        rows, rows, rows, cube, cube, P(("groups", "expert", "replica")), rows,
        P(("expert", "replica"), None), P(), P(("groups", "expert"), None),
        P(("groups", "expert"), None), P("expert", None, "replica"),
        P("expert", None, "replica"), P("expert", "replica", None),
    )
    return jax.shard_map(
        on_device, mesh=mesh, in_specs=in_specs, out_specs=rows, check_vma=False
    )
```

time: 202 us -> 60.3 us (0.30)
  starting transfers between devices: 61.6 us -> 0 us
  waiting for transfers between devices: 56.7 us -> 0 us
  Pallas kernels: 0 us -> 48.7 us
  blocking collectives: 21.6 us -> 0 us
  matrix products: 14.3 us -> 0 us
  other arithmetic: 13.8 us -> 0 us
  between operations: 13.8 us -> 0.03 us
  local copies, waits for them, and re-layouts: 18.3 us -> 10.4 us
    pallas_call x0 -> x1, Pallas kernels: none -> 48.7 us  [on_device(): pl.pallas_call(functools.partial(kernel, E, cap), out_shape=jax.ShapeDtyp...]
    ppermute x14 -> x0, starting transfers between devices: 37.6 us -> none  [shifted(): return lax.ppermute(block, axis, route)]
    all_to_all x3 -> x0, starting transfers between devices: 24 us -> none  [the longest x1 9.28 us: on_device(): lax.all_to_all(repeated, ('expert', 'replica'), split_axis=1, concat_axis...]
    all_to_all x3 -> x0, waiting for transfers between devices: 21.5 us -> none  [the longest x1 15.5 us: on_device(): lax.all_to_all(summed_halves.astype(jnp.bfloat16), 'expert', split_axis=0...]
    all_to_all x1 -> x0, blocking collectives: 19.7 us -> none  [on_device(): lax.all_to_all(outgoing, 'expert', split_axis=0, concat_axis=0, tiled=True)]
    ppermute x14 -> x0, waiting for transfers between devices: 17.8 us -> none  [shifted(): return lax.ppermute(block, axis, route)]
    psum x1 -> x0, waiting for transfers between devices: 17.3 us -> none  [on_device(): lax.psum(partial_value.astype(jnp.bfloat16), 'replica').astype(jnp.float32)]
    dot_general x9 -> x0, matrix products: 14.3 us -> none  [the longest x1 2.77 us: on_device(): gate_act = jnp.dot(slot_rows, w_gate[0], preferred_element_type=jnp.float32)]
  transfers between devices with their start and end apart: 18 -> 0, of which waited for: 7 -> 0; matrix products, arithmetic and copies ran while one was open for 8% -> 0% of each run, Pallas kernels for 0% -> 0%
where the time goes in v1:
time: 60.3 us; the launch traced here: 59.1 us
  Pallas kernels  48.7 us (81%)
  local copies, waits for them, and re-layouts  10.4 us (17%)
    pallas_call x1, Pallas kernels, on_device(): pl.pallas_call(functools.partial(kernel, E, cap), out_shape=jax.ShapeDtyp...  48.7 us
    unnamed x21, local copies, waits for them, and re-layouts  9.65 us

profile of v1, /device:TPU:0, one launch (start us, length us, event | category | flops | bytes accessed | tf_op | source)
XLA Modules:
  0.0 59.1 jit_solution(1894760894286100598)
XLA Ops:
  0.0 0.7 %reshape.3.gain_ref = bf16[1,4096]{1,0:T(2,128)(2,1)S(1)} reshape(bf16[4096]{0:T(1024)(128)(2,1)} %param.22) | data formatting | bytes 16384 | tf_op jit(solution)/shard_map/reshape | solution.py:404
  0.7 0.0 copy-start
  0.7 1.6 %copy-done = bf16[256,4096]{1,0:T(8,128)(2,1)S(1)} copy-done((bf16[256,4096]{1,0:T(8,128)(2,1)S(1)}, bf16[256,4096]{1,0:T(8,128)(2,1)}, u32[]{:S(2)}) %copy-start) | copy-done | bytes 2097176
  2.3 0.0 copy-start.1
  2.3 1.2 %copy-done.1 = bf16[4,256,512]{2,1,0:T(8,128)(2,1)S(1)} copy-done((bf16[4,256,512]{2,1,0:T(8,128)(2,1)S(1)}, bf16[4,256,512]{2,1,0:T(8,128)(2,1)}, u32[]{:S(2)}) %copy-start.1) | copy-done | bytes 1048600
  3.5 0.0 copy-start.2
  3.5 1.2 %copy-done.2 = bf16[4,256,512]{2,1,0:T(8,128)(2,1)S(1)} copy-done((bf16[4,256,512]{2,1,0:T(8,128)(2,1)S(1)}, bf16[4,256,512]{2,1,0:T(8,128)(2,1)}, u32[]{:S(2)}) %copy-start.2) | copy-done | bytes 1048600
  4.8 0.0 copy-start.3
  4.8 0.8 %copy-done.3 = bf16[4,8192]{1,0:T(4,128)(2,1)S(1)} copy-done((bf16[4,8192]{1,0:T(4,128)(2,1)S(1)}, bf16[4,8192]{1,0:T(4,128)(2,1)}, u32[]{:S(2)}) %copy-start.3) | copy-done | bytes 65560
  5.6 0.0 copy-start.4
  5.6 0.8 %copy-done.4 = bf16[4,4096]{1,0:T(4,128)(2,1)S(1)} copy-done((bf16[4,4096]{1,0:T(4,128)(2,1)S(1)}, bf16[4,4096]{1,0:T(4,128)(2,1)}, u32[]{:S(2)}) %copy-start.4) | copy-done | bytes 32792
  6.4 0.0 copy-start.5
  6.4 0.7 %copy-done.5 = bf16[4,512]{1,0:T(4,128)(2,1)S(1)} copy-done((bf16[4,512]{1,0:T(4,128)(2,1)S(1)}, bf16[4,512]{1,0:T(4,128)(2,1)}, u32[]{:S(2)}) %copy-start.5) | copy-done | bytes 4120
  7.0 0.0 copy-start.6
  7.0 0.7 %copy-done.6 = bf16[4,512]{1,0:T(4,128)(2,1)S(1)} copy-done((bf16[4,512]{1,0:T(4,128)(2,1)S(1)}, bf16[4,512]{1,0:T(4,128)(2,1)}, u32[]{:S(2)}) %copy-start.6) | copy-done | bytes 4120
  7.7 0.0 copy-start.7
  7.7 0.7 %copy-done.7 = s32[8,8]{1,0:T(8,128)S(1)} copy-done((s32[8,8]{1,0:T(8,128)S(1)}, s32[8,8]{1,0:T(8,128)}, u32[]{:S(2)}) %copy-start.7) | copy-done | bytes 280
  8.4 0.0 copy-start.8
  8.4 0.7 %copy-done.8 = f32[8,8]{1,0:T(8,128)S(1)} copy-done((f32[8,8]{1,0:T(8,128)S(1)}, f32[8,8]{1,0:T(8,128)}, u32[]{:S(2)}) %copy-start.8) | copy-done | bytes 280
  9.1 0.0 copy-start.9
  9.1 0.7 %copy-done.9 = s32[4]{0:T(128)S(1)} copy-done((s32[4]{0:T(128)S(1)}, s32[4]{0:T(128)}, u32[]{:S(2)}) %copy-start.9) | copy-done | bytes 40
  9.8 48.7 %shard_map.136 = bf16[4,4096]{1,0:T(4,128)(2,1)S(1)} custom-call(bf16[4,8192]{1,0:T(4,128)(2,1)S(1)} %copy-done.3, bf16[4,512]{1,0:T(4,128)(2,1)S(1)} %copy-done.5, bf16[4,512]{1,0:T(4,128)(2,1)S(1)} %copy-done.6, s32[4]{0:T(128)S(1)} %copy-done.9, bf16[4,4096]{1,0:T(4,128)(2,1)S(1)} %copy-done.4, bf16[1,4096]{1,0:T(2,128)(2,1)S(1)} %reshape.3.gain_ref, ...), custom_call_target="tpu_custom_call" | custom-call | tf_op jit(solution)/shard_map/pallas_call | solution.py:394
  58.5 0.6 %copy.16 = bf16[4,4096]{1,0:T(4,128)(2,1)} copy(bf16[4,4096]{1,0:T(4,128)(2,1)S(1)} %shard_map.136) | data formatting | bytes 65536
Async XLA Ops:
  0.7 1.6 %copy-start = (bf16[256,4096]{1,0:T(8,128)(2,1)S(1)}, bf16[256,4096]{1,0:T(8,128)(2,1)}, u32[]{:S(2)}) copy-start(bf16[256,4096]{1,0:T(8,128)(2,1)} %ow_hbm.1) | copy-start | bytes 6291460
  2.3 1.2 %copy-start.1 = (bf16[4,256,512]{2,1,0:T(8,128)(2,1)S(1)}, bf16[4,256,512]{2,1,0:T(8,128)(2,1)}, u32[]{:S(2)}) copy-start(bf16[4,256,512]{2,1,0:T(8,128)(2,1)} %k_hbm.1) | copy-start | bytes 3145732
  3.5 1.2 %copy-start.2 = (bf16[4,256,512]{2,1,0:T(8,128)(2,1)S(1)}, bf16[4,256,512]{2,1,0:T(8,128)(2,1)}, u32[]{:S(2)}) copy-start(bf16[4,256,512]{2,1,0:T(8,128)(2,1)} %v_hbm.1) | copy-start | bytes 3145732
  4.8 0.8 %copy-start.3 = (bf16[4,8192]{1,0:T(4,128)(2,1)S(1)}, bf16[4,8192]{1,0:T(4,128)(2,1)}, u32[]{:S(2)}) copy-start(bf16[4,8192]{1,0:T(4,128)(2,1)} %q_ref.1) | copy-start | bytes 196612
  5.6 0.8 %copy-start.4 = (bf16[4,4096]{1,0:T(4,128)(2,1)S(1)}, bf16[4,4096]{1,0:T(4,128)(2,1)}, u32[]{:S(2)}) copy-start(bf16[4,4096]{1,0:T(4,128)(2,1)} %res_ref.1) | copy-start | bytes 98308
  6.4 0.7 %copy-start.5 = (bf16[4,512]{1,0:T(4,128)(2,1)S(1)}, bf16[4,512]{1,0:T(4,128)(2,1)}, u32[]{:S(2)}) copy-start(bf16[4,512]{1,0:T(4,128)(2,1)} %tk_ref.1) | copy-start | bytes 12292
  7.0 0.7 %copy-start.6 = (bf16[4,512]{1,0:T(4,128)(2,1)S(1)}, bf16[4,512]{1,0:T(4,128)(2,1)}, u32[]{:S(2)}) copy-start(bf16[4,512]{1,0:T(4,128)(2,1)} %tv_ref.1) | copy-start | bytes 12292
  7.7 0.7 %copy-start.7 = (s32[8,8]{1,0:T(8,128)S(1)}, s32[8,8]{1,0:T(8,128)}, u32[]{:S(2)}) copy-start(s32[8,8]{1,0:T(8,128)} %ids_ref.1) | copy-start | bytes 772
  8.4 0.7 %copy-start.8 = (f32[8,8]{1,0:T(8,128)S(1)}, f32[8,8]{1,0:T(8,128)}, u32[]{:S(2)}) copy-start(f32[8,8]{1,0:T(8,128)} %rw_ref.1) | copy-start | bytes 772
  9.1 0.7 %copy-start.9 = (s32[4]{0:T(128)S(1)}, s32[4]{0:T(128)}, u32[]{:S(2)}) copy-start(s32[4]{0:T(128)} %kv_ref.1) | copy-start | bytes 52

commit v2 on v1

--- a/solution.py
+++ b/solution.py
@@ -10,6 +10,7 @@
 
 HEAD_WIDTH = 128
 TILE = 16
+CHUNKS = 1
 MESH = pl.DeviceIdType.MESH
 F32 = jnp.float32
 BF16 = jnp.bfloat16
@@ -30,15 +31,24 @@
     return jnp.dot(a, b, preferred_element_type=F32)
 
 
+def flipped(index, mask, bits):
+    total = 0
+    for k in range(bits):
+        place = 1 << k
+        total = total + lax.rem(lax.div(index, place) + lax.div(mask, place), 2) * place
+    return total
+
+
 def kernel(
     E, cap,
-    q_ref, tk_ref, tv_ref, kv_ref, res_ref, gain_ref, ids_ref, rw_ref,
+    q_hbm, tk_hbm, tv_hbm, kv_hbm, res_hbm, gain_hbm, ids_hbm, rw_hbm,
     k_hbm, v_hbm, ow_hbm, wg_hbm, wu_hbm, wd_hbm,
     out_ref,
+    q_ref, tk_ref, tv_ref, kv_ref, res_ref, gain_ref, ids_ref, rw_ref,
     kb, vb, ow, wg, wu, wd,
     qs, tks, tvs, att, ratt, asm, yb, rs, resb, resp, hs, ssb, ssp,
     tts, whi, wlo, xb, xr, xs, hid, os, zb, zr, ub, up_,
-    lsem, wsem, psend, precv, s1, r1, s2, r2, s3, r3, s4, r4,
+    lsem, osem, wsem, isem, psend, precv, s1, r1, s2, r2, s3, r3, s4, r4,
 ):
     N = 2 * E
     e_me = lax.axis_index("expert")
@@ -59,6 +69,15 @@
     other = pl.ds(pl.multiple_of((1 - c) * half, half), half)
     partner = {"expert": e_me, "replica": 1 - c}
 
+    small = [
+        pltpu.make_async_copy(src, dst, isem.at[k])
+        for k, (src, dst) in enumerate((
+            (q_hbm, q_ref), (tk_hbm, tk_ref), (tv_hbm, tv_ref), (kv_hbm, kv_ref),
+            (res_hbm, res_ref), (gain_hbm, gain_ref), (ids_hbm, ids_ref), (rw_hbm, rw_ref),
+        ))
+    ]
+    for cp in small:
+        cp.start()
     barrier = pltpu.get_barrier_semaphore()
 
     @pl.loop(1, N)
@@ -90,6 +109,8 @@
     for cp in wcopies:
         cp.start()
 
+    for cp in small:
+        cp.wait()
     qf = q_ref[...].astype(F32)
     for h in range(heads):
         qs[pl.ds(S * h, S), :] = qf[:, h * HEAD_WIDTH:(h + 1) * HEAD_WIDTH]
@@ -144,8 +165,13 @@
     def tile(ref, index):
         return ref.at[pl.ds(pl.multiple_of(index * TILE, TILE), TILE)]
 
+    def partner_of(index, i, count, inbound):
+        if count & (count - 1) == 0:
+            return flipped(index, count - i, count.bit_length() - 1)
+        return lax.rem(index + count - i, count) if inbound else lax.rem(index + i, count)
+
     def att_copy(i, inbound=False):
-        peer = lax.rem(rank + N - i, N) if inbound else lax.rem(rank + i, N)
+        peer = partner_of(rank, i, N, inbound)
         who = peer if inbound else rank
         return pltpu.make_async_remote_copy(
             src_ref=tile(att, peer // 2), dst_ref=tile(ratt, who),
@@ -153,14 +179,36 @@
             device_id={"expert": peer // 2, "replica": lax.rem(peer, 2)}, device_id_type=MESH,
         )
 
-    def spread(src, dst, send, recv, i, inbound=False):
-        peer = lax.rem(e_me + E - i, E) if inbound else lax.rem(e_me + i, E)
+    def piece(ref, index, k):
+        wide = ref.shape[-1] // CHUNKS
+        return ref.at[
+            pl.ds(pl.multiple_of(index * TILE, TILE), TILE), pl.ds(k * wide, wide)
+        ]
+
+    def spread(src, dst, send, recv, k, i, inbound=False):
+        peer = partner_of(e_me, i, E, inbound)
         who = peer if inbound else e_me
         return pltpu.make_async_remote_copy(
-            src_ref=tile(src, peer), dst_ref=tile(dst, who),
-            send_sem=send.at[i], recv_sem=recv.at[who],
+            src_ref=piece(src, peer, k), dst_ref=piece(dst, who, k),
+            send_sem=send.at[k, i], recv_sem=recv.at[k, who],
             device_id={"expert": peer, "replica": c}, device_id_type=MESH,
         )
+
+    def scatter(src, dst, send, recv, k, own):
+        @pl.loop(1, E)
+        def _(i):
+            spread(src, dst, send, recv, k, i).start()
+
+        cp = pltpu.make_async_copy(piece(src, e_me, k), piece(dst, e_me, k), osem.at[own, k])
+        cp.start()
+        return cp
+
+    def gather(src, dst, send, recv, k, cp):
+        cp.wait()
+
+        @pl.loop(1, E)
+        def _(i):
+            spread(src, dst, send, recv, k, i, True).wait_recv()
 
     def beside(src, dst, k):
         return pltpu.make_async_remote_copy(
@@ -226,30 +274,24 @@
                 blk[h * 8 * S:(h + 1) * 8 * S]
             )
     quarter = half // 2
-    step = min(512, quarter)
-    for j in range(quarter // step):
+    step = quarter // CHUNKS
+    own2 = []
+    for j in range(CHUNKS):
         y0 = dot(asm[...], ow[:, j * step:(j + 1) * step])
         y1 = dot(asm[...], ow[:, quarter + j * step:quarter + (j + 1) * step])
         both = jnp.concatenate([y0.reshape(E, T, step), y1.reshape(E, T, step)], axis=1)
         yb[:, j * step:(j + 1) * step] = both.reshape(E * TILE, step).astype(BF16)
-
-    @pl.loop(1, E)
-    def _(i):
-        spread(yb, rs, s2, r2, i).start()
-
-    own2 = pltpu.make_async_copy(tile(yb, e_me), tile(rs, e_me), lsem.at[1])
-    own2.start()
+        own2.append(scatter(yb, rs, s2, r2, j, 0))
     res_x.wait()
-    own2.wait()
-
-    @pl.loop(1, E)
-    def _(i):
-        spread(yb, rs, s2, r2, i, True).wait_recv()
-
-    total = rs[0:TILE, :].astype(F32)
-    for j in range(1, E):
-        total = total + rs[j * TILE:(j + 1) * TILE, :].astype(F32)
-    projected = jnp.concatenate([total[:T], total[T:]], axis=1)
+    sums = []
+    for j in range(CHUNKS):
+        gather(yb, rs, s2, r2, j, own2[j])
+        cols = slice(j * step, (j + 1) * step)
+        total = rs[0:TILE, cols].astype(F32)
+        for k in range(1, E):
+            total = total + rs[k * TILE:(k + 1) * TILE, cols].astype(F32)
+        sums.append(total)
+    projected = jnp.concatenate([t[:T] for t in sums] + [t[T:] for t in sums], axis=1)
     trow = lax.broadcasted_iota(jnp.int32, (T, half), 0)
     own_token = trow // S == c
     hidden = jnp.where(own_token, resb[:, mine], resp[...]) + projected
@@ -258,79 +300,81 @@
     ssb[...] = jnp.broadcast_to(square, ssb.shape)
     ss_x = beside(ssb, ssp, 3)
     ss_x.start()
-    scaled = hidden * gain_ref[:, mine].astype(F32)
+    scaled = hidden * gain_ref[mine].astype(F32).reshape(1, half)
     ss_x.wait()
     mean = (square + ssp[:, 0:1]) / D
     normed = scaled * lax.rsqrt(mean + 1e-06)
     stacked = jnp.concatenate([normed[:, p * cw:(p + 1) * cw] for p in range(Q)], axis=0)
-    picked = lax.dot_general(
-        tts[...].astype(BF16), stacked.astype(BF16), (((0,), (0,)), ((), ())),
-        preferred_element_type=F32,
-    )
-    xb[...] = picked.astype(BF16)
-
-    @pl.loop(1, E)
-    def _(i):
-        spread(xb, xr.at[c], s3, r3, i).start()
-
-    own3 = pltpu.make_async_copy(tile(xb, e_me), tile(xr.at[c], e_me), lsem.at[2])
-    own3.start()
+    stacked = stacked.astype(BF16)
+    table = tts[...].astype(BF16)
+    wide = cw // CHUNKS
+    own3 = []
+    for k in range(CHUNKS):
+        picked = lax.dot_general(
+            table, stacked[:, k * wide:(k + 1) * wide], (((0,), (0,)), ((), ())),
+            preferred_element_type=F32,
+        )
+        xb[:, k * wide:(k + 1) * wide] = picked.astype(BF16)
+        own3.append(scatter(xb, xr.at[c], s3, r3, k, 1))
     for cp in wcopies[1:]:
         cp.wait()
     wd_x.wait()
-    own3.wait()
-
-    @pl.loop(1, E)
-    def _(i):
-        spread(xb, xr.at[c], s3, r3, i, True).wait_recv()
-
-    x_x = beside(xr.at[c], xr.at[c], 4)
-    x_x.start()
     px = regroup(Q, cap)
     gc = 8 * cap
-    gate = None
+    gate = jnp.zeros((E * cap, wg.shape[1]), F32)
+    up = gate
+    forwards = []
     for turn in range(2):
         side = c if turn == 0 else 1 - c
-        if turn == 1:
-            x_x.wait()
-        for grp in range(E // 8):
-            blk = dot(px, xr[side, grp * 8 * TILE:(grp + 1) * 8 * TILE, :]).astype(BF16)
+        for k in range(CHUNKS):
+            cols = slice(k * wide, (k + 1) * wide)
+            if turn == 0:
+                gather(xb, xr.at[c], s3, r3, k, own3[k])
+                mid = xr.at[c, :, pl.ds(k * wide, wide)]
+                forwards.append(beside(mid, mid, (4, 7)[k]))
+                forwards[k].start()
+            else:
+                forwards[k].wait()
+            for grp in range(E // 8):
+                blk = dot(px, xr[side, grp * 8 * TILE:(grp + 1) * 8 * TILE, cols]).astype(BF16)
+                for p in range(Q):
+                    xs[turn, grp * gc:(grp + 1) * gc, p * cw + k * wide:p * cw + (k + 1) * wide] = (
+                        blk[p * gc:(p + 1) * gc]
+                    )
             for p in range(Q):
-                xs[turn, grp * gc:(grp + 1) * gc, p * cw:(p + 1) * cw] = blk[p * gc:(p + 1) * gc]
-        feats = pl.ds(pl.multiple_of(side * half, half), half)
-        gpart = dot(xs[turn], wg[feats, :])
-        upart = dot(xs[turn], wu[feats, :])
-        gate, up = (gpart, upart) if turn == 0 else (gate + gpart, up + upart)
+                start = p * cw + k * wide
+                feats = pl.ds(pl.multiple_of(side * half + start, wide), wide)
+                rows_in = xs[turn, :, start:start + wide]
+                gate = gate + dot(rows_in, wg[feats, :])
+                up = up + dot(rows_in, wu[feats, :])
     hid[c] = (gate / (1.0 + jnp.exp(-gate)) * up).astype(BF16)
     h_x = beside(hid.at[c], hid.at[c], 5)
     h_x.start()
     h_x.wait()
-    for p in range(Q):
-        cols = slice(p * cw, (p + 1) * cw)
-        o = dot(hid[0], wd[0:drow, cols]) + dot(hid[1], wd[drow:2 * drow, cols])
-        o = o.astype(BF16)
+    pb = regroup(Q, cap, True)
+    own4 = []
+    for k in range(CHUNKS):
+        mid = slice(k * wide, (k + 1) * wide)
+        for p in range(Q):
+            cols = slice(p * cw + k * wide, p * cw + (k + 1) * wide)
+            o = dot(hid[0], wd[0:drow, cols]) + dot(hid[1], wd[drow:2 * drow, cols])
+            o = o.astype(BF16)
+            for grp in range(E // 8):
+                os[grp * 8 * TILE + p * gc:grp * 8 * TILE + (p + 1) * gc, mid] = (
+                    o[grp * gc:(grp + 1) * gc]
+                )
         for grp in range(E // 8):
-            os[grp * 8 * TILE + p * gc:grp * 8 * TILE + (p + 1) * gc, :] = (
-                o[grp * gc:(grp + 1) * gc]
-            )
-    pb = regroup(Q, cap, True)
-    for grp in range(E // 8):
-        part = slice(grp * 8 * TILE, (grp + 1) * 8 * TILE)
-        zb[part, :] = dot(pb, os[part, :]).astype(BF16)
-
-    @pl.loop(1, E)
-    def _(i):
-        spread(zb, zr, s4, r4, i).start()
-
-    own4 = pltpu.make_async_copy(tile(zb, e_me), tile(zr, e_me), lsem.at[3])
-    own4.start()
-    own4.wait()
-
-    @pl.loop(1, E)
-    def _(i):
-        spread(zb, zr, s4, r4, i, True).wait_recv()
-
-    moe = dot(whi[...].astype(BF16), zr[...]) + dot(wlo[...].astype(BF16), zr[...])
+            part = slice(grp * 8 * TILE, (grp + 1) * 8 * TILE)
+            zb[part, mid] = dot(pb, os[part, mid]).astype(BF16)
+        own4.append(scatter(zb, zr, s4, r4, k, 2))
+    parts = []
+    for k in range(CHUNKS):
+        mid = slice(k * wide, (k + 1) * wide)
+        gather(zb, zr, s4, r4, k, own4[k])
+        parts.append(
+            dot(whi[...].astype(BF16), zr[:, mid]) + dot(wlo[...].astype(BF16), zr[:, mid])
+        )
+    moe = jnp.concatenate(parts, axis=1)
     updated = hs[...] + jnp.concatenate([moe[p * T:(p + 1) * T] for p in range(Q)], axis=1)
     ub[...] = updated
     u_x = beside(ub, up_, 6)
@@ -347,9 +391,10 @@
 
     @pl.loop(1, E)
     def _(i):
-        spread(yb, rs, s2, r2, i).wait_send()
-        spread(xb, xr.at[c], s3, r3, i).wait_send()
-        spread(zb, zr, s4, r4, i).wait_send()
+        for k in range(CHUNKS):
+            spread(yb, rs, s2, r2, k, i).wait_send()
+            spread(xb, xr.at[c], s3, r3, k, i).wait_send()
+            spread(zb, zr, s4, r4, k, i).wait_send()
 
 
 def on_device(
@@ -371,11 +416,12 @@
     cw = half // Q
     orow = out_weight.shape[0]
     vmem = pl.BlockSpec(memory_space=pltpu.VMEM)
-    smem = pl.BlockSpec(memory_space=pltpu.SMEM)
-    hbm = pl.BlockSpec(memory_space=pl.ANY)
+    hbm = pl.BlockSpec(memory_space=pltpu.HBM)
     V = pltpu.VMEM
     dma = pltpu.SemaphoreType.DMA
     scratch = [
+        V((S, features), BF16), V((S, KW), BF16), V((S, KW), BF16), pltpu.SMEM((S,), jnp.int32),
+        V((S, D), BF16), V((D,), BF16), V(expert_ids.shape, jnp.int32), V(route_weight.shape, F32),
         V((S * L, KW), BF16), V((S * L, KW), BF16),
         V((2 * orow, half), BF16), V((D, FH), BF16), V((D, FH), BF16), V((2 * FH, half), BF16),
         V((S * features // HEAD_WIDTH, HEAD_WIDTH), F32), V((8, KW), F32), V((8, KW), F32),
@@ -388,20 +434,20 @@
         V((2, E * cap, FH), BF16),
         V((E * TILE, cw), BF16), V((E * TILE, cw), BF16), V((E * TILE, cw), BF16),
         V((T, half), F32), V((T, half), F32),
-        dma((2 * S,)), dma((4,)), dma((7,)), dma((7,)),
-        dma((N,)), dma((N,)), dma((E,)), dma((E,)), dma((E,)), dma((E,)), dma((E,)), dma((E,)),
+        dma((2 * S,)), dma((3, CHUNKS)), dma((4,)), dma((8,)), dma((8,)), dma((8,)),
+        dma((N,)), dma((N,)), *[dma((CHUNKS, E))] * 6,
     ]
     return pl.pallas_call(
         functools.partial(kernel, E, cap),
         out_shape=jax.ShapeDtypeStruct((S, D), BF16),
-        in_specs=[vmem, vmem, vmem, smem, vmem, vmem, vmem, vmem, hbm, hbm, hbm, hbm, hbm, hbm],
+        in_specs=[hbm] * 14,
         out_specs=vmem,
         scratch_shapes=scratch,
         compiler_params=pltpu.CompilerParams(
-            collective_id=0, has_side_effects=True, vmem_limit_bytes=48 * 1024 * 1024
+            collective_id=0, has_side_effects=True, vmem_limit_bytes=67043328
         ),
     )(
-        queries, token_keys, token_values, kv_len, residual, norm_gain.reshape(1, D), expert_ids,
+        queries, token_keys, token_values, kv_len, residual, norm_gain, expert_ids,
         route_weight, stored_keys, stored_values, out_weight, w_gate, w_up, w_down,
     )
 

time: 60.3 us -> 53.1 us (0.88); the launches traced: 59.1 us -> 52.9 us
  local copies, waits for them, and re-layouts: 10.4 us -> 1.39 us
  Pallas kernels: 48.7 us -> 51.5 us
    unnamed x21 -> x1, local copies, waits for them, and re-layouts: 9.65 us -> 1.39 us
    pallas_call x1, Pallas kernels: 48.7 us -> 51.5 us  [on_device(): pl.pallas_call(functools.partial(kernel, E, cap), out_shape=jax.ShapeDtyp...]
    reshape x1 -> x0, local copies, waits for them, and re-layouts: 0.71 us -> none  [on_device(): norm_gain.reshape(1, D)]
where the time goes in v2:
time: 53.1 us; the launch traced here: 52.9 us
  Pallas kernels  51.5 us (97%)
  local copies, waits for them, and re-layouts  1.39 us (3%)
    pallas_call x1, Pallas kernels, on_device(): pl.pallas_call(functools.partial(kernel, E, cap), out_shape=jax.ShapeDtyp...  51.5 us
    unnamed x1, local copies, waits for them, and re-layouts  1.39 us

profile of v2, /device:TPU:0, one launch (start us, length us, event | category | flops | bytes accessed | tf_op | source)
XLA Modules:
  0.0 52.9 jit_solution(1963616420592121500)
XLA Ops:
  0.0 51.5 %shard_map.136 = bf16[4,4096]{1,0:T(4,128)(2,1)} custom-call(bf16[4,8192]{1,0:T(4,128)(2,1)} %q_hbm.1, bf16[4,512]{1,0:T(4,128)(2,1)} %tk_hbm.1, bf16[4,512]{1,0:T(4,128)(2,1)} %tv_hbm.1, s32[4]{0:T(128)} %kv_hbm.1, bf16[4,4096]{1,0:T(4,128)(2,1)} %res_hbm.1, bf16[4096]{0:T(1024)(128)(2,1)} %gain_hbm.1, s32[8,8]{1,0:T(8,128)} %ids_hbm.1, f32[8,8]{1,0:T(8,128)} %rw_hbm.1, ...), custom_call_target="tpu_custom_call" | custom-call | tf_op jit(solution)/shard_map/pallas_call | solution.py:440
  51.5 1.4 %copy.16 = bf16[4,4096]{1,0:T(4,128)(2,1)} copy(bf16[4,4096]{1,0:T(4,128)(2,1)} %shard_map.136) | data formatting | bytes 65536
